TPU v7x, 32 devices: a whole 2x2x4 slice. The times are simulated.
32 devices in a mesh: grp: 4 (over z), ctx: 2 (over y), wid: 4 (over x, core).
Axes of the slice: x: 2, y: 2, z: 4, core: 2. Of those that a mesh axis runs over, the one named last changes fastest.
Arguments:
- query: bfloat16 [256, 64, 128], P(None, 'wid'), may hold values from -64 to 64
- keys: bfloat16 [4, 512, 8, 128], P(None, ('grp', 'ctx'), 'wid'), may hold values from -64 to 64
- values: bfloat16 [4, 512, 8, 128], P(None, ('grp', 'ctx'), 'wid'), may hold values from -6 to 6
- lengths: int32 [4, 8], replicated, may hold values from 32 to 64
- query_pos: int32 [256], replicated, may hold values from 128 to 511
- resid: bfloat16 [256, 5120], P('wid', ('grp', 'ctx')), may hold values from -1.1953125 to 1.1953125
- out_weight: bfloat16 [8192, 5120], P('wid', ('grp', 'ctx')), may hold values from -0.0625 to 0.0625
- enc_weight: bfloat16 [5120, 24576], P('wid', ('grp', 'ctx')), may hold values from -0.078125 to 0.078125
- enc_bias: float32 [24576], P(('grp', 'ctx')), may hold values from -3 to 3
- dec_weight: bfloat16 [24576, 5120], P(('grp', 'ctx'), 'wid'), may hold values from -0.078125 to 0.078125
- dec_bias: float32 [5120], P('wid'), may hold values from -3 to 3
Outputs:
- layer_out: bfloat16 [256, 5120], P('wid', ('grp', 'ctx'))
- enc_grad: bfloat16 [5120, 24576], P('wid', ('grp', 'ctx'))
- enc_bias_grad: float32 [24576], P(('grp', 'ctx'))
- dec_grad: bfloat16 [24576, 5120], P(('grp', 'ctx'), 'wid')
- dec_bias_grad: float32 [5120], P('wid')
Inputs may be any that keep to these rules, and one draw needn't show every extreme that they name: `lengths`: live slots of a shard are its first ones.
All inputs are finite; a program needn't handle non-finite values.
Results may differ from a plain program's by a relative error of at most 0.024.
Values may be sent and summed in bfloat16 or wider, within the bound.
A program may use at most 128 MiB of HBM per device.

v0:
```python
import jax
import jax.numpy as jnp
from jax import lax
from jax.sharding import PartitionSpec as P

HD = 128


def body(
    query,
    keys,
    values,
    lengths,
    query_pos,
    resid,
    out_weight,
    enc_weight,
    enc_bias,
    dec_weight,
    dec_bias,
):
    seq_count, slot_count, kv_local, head_dim = keys.shape
    row_count = query.shape[0]
    heads_local = query.shape[1]
    group_size = heads_local // kv_local
    rows_each = row_count // seq_count
    shard_pos = lax.axis_index(("grp", "ctx"))
    shard_ids = jnp.arange(lengths.shape[1], dtype=jnp.int32)
    offset = jnp.sum(jnp.where(shard_ids[None, :] < shard_pos, lengths, 0), axis=1)
    live_count = jnp.sum(jnp.where(shard_ids[None, :] == shard_pos, lengths, 0), axis=1)
    slot_ids = jnp.arange(slot_count, dtype=jnp.int32)
    key_pos = offset[:, None] + slot_ids[None, :]
    live_slot = slot_ids[None, :] < live_count[:, None]
    row_position = query_pos.reshape(seq_count, rows_each)
    visible = live_slot[:, None, :] & (key_pos[:, None, :] <= row_position[:, :, None])
    visible_mask = visible[:, :, None, None, :]
    q_view = query.reshape(seq_count, rows_each, kv_local, group_size, head_dim)
    scores = jnp.einsum(
        "srkgd,sjkd->srkgj", q_view, keys, preferred_element_type=jnp.float32
    ) * HD ** (-0.5)
    local_peak = jnp.max(jnp.where(visible_mask, scores, -1e30), axis=-1)
    peak = lax.pmax(local_peak, ("grp", "ctx"))
    weights = jnp.where(visible_mask, jnp.exp(scores - peak[..., None]), 0.0)
    weight_sum = jnp.sum(weights, axis=-1)
    weights_low = weights.astype(jnp.bfloat16)
    weighted = jnp.einsum(
        "srkgj,sjkd->srkgd", weights_low, values, preferred_element_type=jnp.float32
    )
    weight_sum, weighted = (weight_sum, weighted)
    weight_sum, weighted = lax.psum((weight_sum, weighted), ("grp", "ctx"))
    attention = (weighted / weight_sum[..., None]).astype(jnp.bfloat16)
    attention = attention.reshape(row_count, heads_local * head_dim)
    projected = jnp.dot(attention, out_weight, preferred_element_type=jnp.float32)
    mixed = lax.psum_scatter(
        projected.astype(jnp.bfloat16), "wid", scatter_dimension=0, tiled=True
    ).astype(jnp.float32)
    layer_out = (mixed + resid.astype(jnp.float32)).astype(jnp.bfloat16)
    wide_rows = lax.all_gather(layer_out, ("grp", "ctx"), axis=1, tiled=True)
    block = lax.all_to_all(wide_rows, "wid", split_axis=1, concat_axis=0, tiled=True)
    enc_part = jnp.dot(block, enc_weight, preferred_element_type=jnp.float32)
    preact = lax.psum(enc_part.astype(jnp.bfloat16), "wid").astype(jnp.float32) + enc_bias
    latents = (jax.nn.softplus(4.0 * preact) * 0.25).astype(jnp.bfloat16)
    row_scale = row_count ** (-0.5)
    recon = lax.psum_scatter(
        jnp.dot(latents, dec_weight, preferred_element_type=jnp.float32),
        ("grp", "ctx"),
        scatter_dimension=0,
        tiled=True,
    )
    piece_len = recon.shape[0]
    target = lax.dynamic_slice_in_dim(block, shard_pos * piece_len, piece_len, 0).astype(
        jnp.float32
    )
    scaled_error = ((recon + dec_bias - target) * row_scale).astype(jnp.bfloat16)
    error_all = lax.all_gather(scaled_error, ("grp", "ctx"), axis=0, tiled=True)
    dec_bias_grad = jnp.sum(error_all, axis=0, dtype=jnp.float32)
    latent_part = lax.dot_general(
        error_all, dec_weight, (((1,), (1,)), ((), ())), preferred_element_type=jnp.float32
    )
    dec_grad = lax.dot_general(
        latents, error_all, (((0,), (0,)), ((), ())), preferred_element_type=jnp.float32
    )
    latent_grad = lax.psum(latent_part.astype(jnp.bfloat16), "wid").astype(jnp.float32)
    preact_grad = (latent_grad * jax.nn.sigmoid(4.0 * preact)).astype(jnp.bfloat16)
    enc_grad = lax.dot_general(
        block, preact_grad, (((0,), (0,)), ((), ())), preferred_element_type=jnp.float32
    ).astype(jnp.bfloat16)
    enc_bias_grad = jnp.sum(preact_grad, axis=0, dtype=jnp.float32)
    return (layer_out, enc_grad, enc_bias_grad, dec_grad.astype(jnp.bfloat16), dec_bias_grad)


def solution(mesh):
    placed = (
        P(None, "wid", None),
        P(None, ("grp", "ctx"), "wid", None),
        P(None, ("grp", "ctx"), "wid", None),
        P(),
        P(),
        P("wid", ("grp", "ctx")),
        P("wid", ("grp", "ctx")),
        P("wid", ("grp", "ctx")),
        P(("grp", "ctx")),
        P(("grp", "ctx"), "wid"),
        P("wid"),
    )
    return jax.shard_map(
        body,
        mesh=mesh,
        in_specs=placed,
        out_specs=(
            P("wid", ("grp", "ctx")),
            P("wid", ("grp", "ctx")),
            P(("grp", "ctx")),
            P(("grp", "ctx"), "wid"),
            P("wid"),
        ),
        check_vma=False,
    )
```

profile of v0, /device:TPU:0, one launch (start us, length us, event | category | flops | bytes accessed | tf_op | source)
XLA Modules:
  0.0 456.0 jit_solution(1669517848478432027)
XLA Ops:
  7.2 0.9 le.20
  8.1 0.8 select_reduce_fusion.1
  9.1 0.1 compare_and_fusion
  9.3 3.8 fusion.2
  13.0 39.0 %pmax.7 = f32[4,64,2,8]{1,3,2,0:T(8,128)S(1)} all-reduce(f32[4,64,2,8]{1,3,2,0:T(8,128)S(1)} %get-tuple-element.11), channel_id=1, replica_groups=mesh['grp'=4,'ctx'=2,'wid'=4] {'grp','ctx'}, use_global_device_ids=true, to_apply=%region_3.4 | all-reduce | flops 4096 | bytes 32768 | tf_op jit(solution)/shard_map/pmax | solution.py:42
  52.0 3.2 fusion.5
  55.3 2.4 copy.29
  57.7 3.0 convolution_bitcast_fusion
  60.7 34.2 %psum.29 = f32[4,64,2,8]{1,3,2,0:T(8,128)S(1)} all-reduce(f32[4,64,2,8]{1,3,2,0:T(8,128)S(1)} %get-tuple-element.9), channel_id=1, replica_groups=mesh['grp'=4,'ctx'=2,'wid'=4] {'grp','ctx'}, use_global_device_ids=true, to_apply=%region_6.7 | all-reduce | flops 4096 | bytes 32768 | tf_op jit(solution)/shard_map/psum | solution.py:50
  94.9 0.1 copy.31
  95.0 65.7 %all-reduce.4.cloned.1.call-done = f32[4,64,2,8,128]{4,3,1,2,0:T(8,128)} async-done(((f32[4,64,2,8,128]{4,3,1,2,0:T(8,128)}), f32[4,64,2,8,128]{4,3,1,2,0:T(8,128)}) %all-reduce.4.cloned.1.call-update) | async-done | bytes 2097168 | tf_op jit(solution)/shard_map/psum | solution.py:50
  160.8 1.9 divide_convert_fusion
  162.7 1.2 copy.32
  163.9 2.3 reshape.71
  166.2 2.9 convolution_convert_fusion.4
  169.2 19.8 %reduce-scatter.3.cloned.1.call-done = bf16[64,640]{1,0:T(8,128)(2,1)} async-done(((bf16[256,640]{1,0:T(8,128)(2,1)}), bf16[64,640]{1,0:T(8,128)(2,1)}) %reduce-scatter.3.cloned.1.call-update) | async-done | bytes 81936 | tf_op jit(solution)/shard_map/reduce_scatter | solution.py:54
  189.0 0.9 add_convert_fusion
  189.9 32.1 %all_gather.6 = bf16[64,5120]{1,0:T(8,128)(2,1)S(1)} all-gather(bf16[64,640]{1,0:T(8,128)(2,1)S(1)} %add_convert_fusion), channel_id=1, replica_groups=mesh['grp'=4,'ctx'=2,'wid'=4] {'grp','ctx'}, dimensions={1}, use_global_device_ids=true | all-gather | bytes 737280 | tf_op jit(solution)/shard_map/all_gather | solution.py:58
  222.1 12.6 %all_to_all.19 = bf16[64,4,1280]{2,0,1:T(8,128)(2,1)S(1)} all-to-all(bf16[64,4,1280]{2,0,1:T(8,128)(2,1)S(1)} %bitcast.41), channel_id=1, replica_groups=mesh['grp'=4,'ctx'=2,'wid'=4] {'wid'}, dimensions={1} | all-to-all | bytes 1310720 | tf_op jit(solution)/shard_map/all_to_all | solution.py:59
  234.7 6.6 %convolution_convert_fusion.3 = bf16[256,3072]{1,0:T(8,128)(2,1)} fusion(bf16[256,1280]{1,0:T(8,128)(2,1)S(1)} %bitcast.38, bf16[1280,3072]{1,0:T(8,128)(2,1)} %param.18), kind=kOutput, calls=%fused_computation.4 | convolution fusion | flops 2014052352 | bytes 10092544 | tf_op jit(solution)/shard_map/dot_general | solution.py:60
  241.4 42.7 %all-reduce.6.cloned.1.call-done = bf16[256,3072]{1,0:T(8,128)(2,1)} async-done(((bf16[256,3072]{1,0:T(8,128)(2,1)}), bf16[256,3072]{1,0:T(8,128)(2,1)}) %all-reduce.6.cloned.1.call-update) | async-done | bytes 1572880 | tf_op jit(solution)/shard_map/psum | solution.py:61
  284.1 8.8 %fusion.12 = f32[256,1280]{1,0:T(8,128)} fusion(bf16[3072,1280]{1,0:T(8,128)(2,1)} %param.20, bf16[256,3072]{1,0:T(8,128)(2,1)} %all-reduce.6.cloned.1.call-done, f32[3072]{0:T(1024)S(1)} %copy-done.5), kind=kOutput, calls=%fused_computation.35 | convolution fusion | flops 2021916672 | bytes 10760192 | tf_op jit(solution)/shard_map/dot_general | solution.py:65
  293.0 65.3 %reduce-scatter.5.cloned.1.call-done = f32[32,1280]{1,0:T(8,128)} async-done(((f32[256,1280]{1,0:T(8,128)}), f32[32,1280]{1,0:T(8,128)}) %reduce-scatter.5.cloned.1.call-update) | async-done | bytes 163856 | tf_op jit(solution)/shard_map/reduce_scatter | solution.py:64
  358.3 0.9 multiply_convert_fusion.1
  359.2 32.1 %all_gather.7 = bf16[256,1280]{1,0:T(8,128)(2,1)S(1)} all-gather(bf16[32,1280]{1,0:T(8,128)(2,1)S(1)} %multiply_convert_fusion.1), channel_id=1, replica_groups=mesh['grp'=4,'ctx'=2,'wid'=4] {'grp','ctx'}, dimensions={0}, use_global_device_ids=true | all-gather | bytes 737280 | tf_op jit(solution)/shard_map/all_gather | solution.py:75
  391.4 0.8 copy-done.1
  392.2 6.6 %convolution_convert_fusion.2 = bf16[256,3072]{1,0:T(8,128)(2,1)} fusion(bf16[256,1280]{1,0:T(8,128)(2,1)S(1)} %all_gather.7, bf16[3072,1280]{1,0:T(8,128)(2,1)} %param.20), kind=kOutput, calls=%fused_computation.3 | convolution fusion | flops 2014052352 | bytes 10092544 | tf_op jit(solution)/shard_map/dot_general | solution.py:77
  398.8 1.8 convert_reduce_fusion.1
  400.6 9.0 %convolution_convert_fusion = bf16[3072,1280]{1,0:T(8,128)(2,1)} fusion(bf16[256,1280]{1,0:T(8,128)(2,1)} %copy-done.1, bf16[256,3072]{1,0:T(8,128)(2,1)} %all-reduce.6.cloned.1.call-done, f32[3072]{0:T(1024)S(1)} %copy-done.5), kind=kOutput, calls=%fused_computation | convolution fusion | flops 2025848832 | bytes 10104832 | tf_op jit(solution)/shard_map/dot_general | solution.py:80
  409.6 30.8 %all-reduce.8.cloned.1.call-done = bf16[256,3072]{1,0:T(8,128)(2,1)} async-done(((bf16[256,3072]{1,0:T(8,128)(2,1)}), bf16[256,3072]{1,0:T(8,128)(2,1)}) %all-reduce.8.cloned.1.call-update) | async-done | bytes 1572880 | tf_op jit(solution)/shard_map/psum | solution.py:83
  440.4 3.6 convert_reduce_fusion
  444.0 5.5 %convolution_convert_fusion.1 = bf16[1280,3072]{1,0:T(8,128)(2,1)} fusion(bf16[256,1280]{1,0:T(8,128)(2,1)S(1)} %bitcast.40, bf16[256,3072]{1,0:T(8,128)(2,1)S(1)} %get-tuple-element.8), kind=kOutput, calls=%fused_computation.1 | convolution fusion | flops 2017198080 | bytes 10092544 | tf_op jit(solution)/shard_map/dot_general | solution.py:85
  (27 shorter events, 0.5 us)
Async XLA Ops:
  7.2 159.0 %copy-start = (bf16[2048,640]{1,0:T(8,128)(2,1)S(1)}, bf16[2048,640]{1,0:T(8,128)(2,1)}, u32[]{:S(2)}) copy-start(bf16[2048,640]{1,0:T(8,128)(2,1)} %param.17) | copy-start | bytes 7864324
  7.2 153.6 %all-reduce.4.cloned.1.call-start = ((), (), s32[]{:S(2)}) async-start(), calls=%async_computation.3 | async-start | bytes 4194304 | tf_op jit(solution)/shard_map/psum | solution.py:50
  13.0 44.6 %copy-start.3 = (bf16[4,64,2,128]{3,2,1,0:T(2,128)(2,1)S(1)}, bf16[4,64,2,128]{3,2,1,0:T(2,128)(2,1)}, u32[]{:S(2)}) copy-start(bf16[4,64,2,128]{3,2,1,0:T(2,128)(2,1)} %param.13) | copy-start | bytes 393220
  60.7 128.4 %reduce-scatter.3.cloned.1.call-start = ((), (), s32[]{:S(2)}) async-start(), calls=%async_computation.4 | async-start | bytes 409600 | tf_op jit(solution)/shard_map/reduce_scatter | solution.py:54
  163.9 25.1 %copy-start.4 = (bf16[64,640]{1,0:T(8,128)(2,1)S(1)}, bf16[64,640]{1,0:T(8,128)(2,1)}, u32[]{:S(2)}) copy-start(bf16[64,640]{1,0:T(8,128)(2,1)} %param.16) | copy-start | bytes 245764
  169.1 114.9 %all-reduce.6.cloned.1.call-start = ((), (), s32[]{:S(2)}) async-start(), calls=%async_computation.5 | async-start | bytes 3145728 | tf_op jit(solution)/shard_map/psum | solution.py:61
  189.9 51.4 %copy-start.2 = (bf16[64,640]{1,0:T(8,128)(2,1)}, bf16[64,640]{1,0:T(8,128)(2,1)S(1)}, u32[]{:S(2)}) copy-start(bf16[64,640]{1,0:T(8,128)(2,1)S(1)} %add_convert_fusion) | copy-start | bytes 245764
  234.7 49.3 %copy-start.5 = (f32[3072]{0:T(1024)S(1)}, f32[3072]{0:T(1024)}, u32[]{:S(2)}) copy-start(f32[3072]{0:T(1024)} %param.19) | copy-start | bytes 36868
  241.4 116.9 %copy-start.6 = (f32[1280]{0:T(1024)S(1)}, f32[1280]{0:T(1024)}, u32[]{:S(2)}) copy-start(f32[1280]{0:T(1024)} %param.21) | copy-start | bytes 15364
  241.4 116.9 %reduce-scatter.5.cloned.1.call-start = ((), (), s32[]{:S(2)}) async-start(), calls=%async_computation.6 | async-start | bytes 1474560 | tf_op jit(solution)/shard_map/reduce_scatter | solution.py:64
  293.0 147.5 %all-reduce.8.cloned.1.call-start = ((), (), s32[]{:S(2)}) async-start(), calls=%async_computation.7 | async-start | bytes 3145728 | tf_op jit(solution)/shard_map/psum | solution.py:83
  391.4 0.8 copy-start.1
Sparse Core Ops, SparseCore 0:
  60.8 99.9 all-reduce.3
  169.3 19.6 reduce-scatter.2
  241.5 42.5 all-reduce.5
  293.1 65.1 reduce-scatter.4
  398.9 41.4 all-reduce.7
where the time goes:
time: 457 us; the launch traced here: 456 us
  waiting for transfers between devices  224 us (49%)
  blocking collectives  150 us (33%)
  matrix products  46.2 us (10%)
  between operations  13.9 us (3%)
  other arithmetic  13.5 us (3%)
  local copies, waits for them, and re-layouts  7.82 us (2%)
    psum x1, waiting for transfers between devices, body(): weight_sum, weighted = lax.psum((weight_sum, weighted), ('grp', 'ctx'))  65.7 us
    reduce_scatter x1, waiting for transfers between devices, body(): lax.psum_scatter(jnp.dot(latents, dec_weight, preferred_element_type=jnp....  65.3 us
    psum x1, waiting for transfers between devices, body(): lax.psum(enc_part.astype(jnp.bfloat16), 'wid').astype(jnp.float32)  42.7 us
    pmax x1, blocking collectives, body(): peak = lax.pmax(local_peak, ('grp', 'ctx'))  39 us
    psum x1, blocking collectives, body(): weight_sum, weighted = lax.psum((weight_sum, weighted), ('grp', 'ctx'))  34.2 us
    all_gather x1, blocking collectives, body(): wide_rows = lax.all_gather(layer_out, ('grp', 'ctx'), axis=1, tiled=True)  32.1 us
    all_gather x1, blocking collectives, body(): error_all = lax.all_gather(scaled_error, ('grp', 'ctx'), axis=0, tiled=True)  32.1 us
    psum x1, waiting for transfers between devices, body(): lax.psum(latent_part.astype(jnp.bfloat16), 'wid').astype(jnp.float32)  30.8 us
  transfers between devices with their start and end apart: 5, of which 5 were waited for; matrix products, arithmetic and copies ran while one was open for 2% of the time, Pallas kernels for 0%

commit v1 on v0

v1 whole, which is shorter than its diff:
```python
import functools

import jax
import jax.numpy as jnp
from jax import lax
from jax.experimental import pallas as pl
from jax.experimental.pallas import tpu as pltpu
from jax.sharding import PartitionSpec as P

HD = 128
MESH = pl.DeviceIdType.MESH


def exchange_kernel(n, where, peer_id, gather, x_ref, out_ref, send_sem, recv_sem):
    me = where()
    peers = [lax.rem(me + step, n) for step in range(1, n)]
    barrier = pltpu.get_barrier_semaphore()
    for peer in peers:
        pl.semaphore_signal(barrier, inc=1, device_id=peer_id(peer), device_id_type=MESH)
    pl.semaphore_wait(barrier, n - 1)

    def copy_to(step, peer):
        return pltpu.make_async_remote_copy(
            src_ref=x_ref if gather else x_ref.at[peer],
            dst_ref=out_ref.at[me],
            send_sem=send_sem.at[step],
            recv_sem=recv_sem.at[me],
            device_id=peer_id(peer),
            device_id_type=MESH,
        )

    def copy_from(step, peer):
        return pltpu.make_async_remote_copy(
            src_ref=x_ref if gather else x_ref.at[peer],
            dst_ref=out_ref.at[peer],
            send_sem=send_sem.at[step],
            recv_sem=recv_sem.at[peer],
            device_id=peer_id(peer),
            device_id_type=MESH,
        )

    sends = [copy_to(step, peer) for step, peer in enumerate(peers)]
    for copy in sends:
        copy.start()
    out_ref[me] = x_ref[...] if gather else x_ref[me]
    for step, peer in enumerate(peers):
        copy_from(step, peer).wait_recv()
    for copy in sends:
        copy.wait_send()


def exchange(x, n, where, peer_id, gather, number):
    block = x.shape if gather else x.shape[1:]
    return pl.pallas_call(
        functools.partial(exchange_kernel, n, where, peer_id, gather),
        out_shape=jax.ShapeDtypeStruct((n,) + block, x.dtype),
        in_specs=[pl.BlockSpec(memory_space=pltpu.VMEM)],
        out_specs=pl.BlockSpec(memory_space=pltpu.VMEM),
        scratch_shapes=[pltpu.SemaphoreType.DMA((n,)), pltpu.SemaphoreType.DMA((n,))],
        compiler_params=pltpu.CompilerParams(
            collective_id=number, has_side_effects=True, vmem_limit_bytes=24 * 1024 * 1024
        ),
        name="exchange%d" % number,
    )(x)


class Groups:
    def __init__(self, sizes):
        ctx_n = sizes["ctx"]
        self.shards = (
            sizes["grp"] * ctx_n,
            lambda: lax.axis_index("grp") * ctx_n + lax.axis_index("ctx"),
            lambda p: {"grp": p // ctx_n, "ctx": lax.rem(p, ctx_n)},
        )
        self.wid = (sizes["wid"], lambda: lax.axis_index("wid"), lambda p: {"wid": p})
        self.low = (
            2,
            lambda: lax.rem(lax.axis_index("wid"), 2),
            lambda p: {"wid": (lax.axis_index("wid") // 2) * 2 + p},
        )
        self.high = (
            sizes["wid"] // 2,
            lambda: lax.axis_index("wid") // 2,
            lambda p: {"wid": p * 2 + lax.rem(lax.axis_index("wid"), 2)},
        )


def scatter_sum(x, group, number):
    n = group[0]
    parts = exchange(x.reshape((n, x.shape[0] // n) + x.shape[1:]), *group, False, number)
    return jnp.sum(parts.astype(jnp.float32), axis=0)


def gather_rows(x, group, number):
    whole = exchange(x, *group, True, number)
    return whole.reshape((whole.shape[0] * whole.shape[1],) + whole.shape[2:])


def attend(groups, query, keys, values, lengths, query_pos):
    seq_count, slot_count, kv_local, head_dim = keys.shape
    row_count, heads_local = query.shape[:2]
    group_size = heads_local // kv_local
    shards = groups.shards[0]
    pairs = seq_count * kv_local
    chunks = shards // pairs
    rows = row_count // seq_count // chunks
    pair = lax.axis_index(("grp", "ctx")) // chunks
    seq, head = pair // kv_local, lax.rem(pair, kv_local)
    row0 = seq * (row_count // seq_count) + lax.rem(lax.axis_index(("grp", "ctx")), chunks) * rows
    cache = jnp.concatenate([keys, values], axis=-1).transpose(0, 2, 1, 3)
    cache = cache.reshape(pairs, slot_count, 2 * head_dim)
    if chunks > 1:
        cache = jnp.repeat(cache, chunks, axis=0)
    cache = exchange(cache, *groups.shards, False, 0).reshape(shards * slot_count, 2 * head_dim)
    q = lax.dynamic_slice(query, (row0, head * group_size, 0), (rows, group_size, head_dim))
    live = lax.dynamic_index_in_dim(lengths, seq, 0, keepdims=False)
    before = jnp.arange(shards)[None, :] < jnp.arange(shards)[:, None]
    offset = jnp.sum(jnp.where(before, live[None, :], 0), axis=1)
    slot_ids = jnp.arange(slot_count, dtype=jnp.int32)
    key_pos = jnp.where(
        slot_ids[None, :] < live[:, None], offset[:, None] + slot_ids[None, :], jnp.int32(2**30)
    ).reshape(-1)
    position = lax.dynamic_slice_in_dim(query_pos, row0, rows, 0)
    visible = (key_pos[None, :] <= position[:, None])[:, None, :]
    scores = jnp.einsum(
        "rgd,td->rgt", q, cache[:, :head_dim], preferred_element_type=jnp.float32
    ) * HD ** (-0.5)
    peak = jnp.max(jnp.where(visible, scores, -1e30), axis=-1, keepdims=True)
    weights = jnp.where(visible, jnp.exp(scores - peak), 0.0)
    weight_sum = jnp.sum(weights, axis=-1, keepdims=True)
    weighted = jnp.einsum(
        "rgt,td->rgd", weights.astype(jnp.bfloat16), cache[:, head_dim:],
        preferred_element_type=jnp.float32,
    )
    mine = (weighted / weight_sum).astype(jnp.bfloat16).reshape(rows, group_size * head_dim)
    attention = exchange(mine, *groups.shards, True, 1)
    attention = attention.reshape(seq_count, kv_local, chunks, rows, group_size * head_dim)
    return attention.transpose(0, 2, 3, 1, 4).reshape(row_count, heads_local * head_dim)


def body(
    sizes,
    query,
    keys,
    values,
    lengths,
    query_pos,
    resid,
    out_weight,
    enc_weight,
    enc_bias,
    dec_weight,
    dec_bias,
):
    groups = Groups(sizes)
    row_count = query.shape[0]
    shard_pos = lax.axis_index(("grp", "ctx"))
    attention = attend(groups, query, keys, values, lengths, query_pos)
    projected = jnp.dot(attention, out_weight, preferred_element_type=jnp.float32)
    mixed = scatter_sum(projected.astype(jnp.bfloat16), groups.wid, 2)
    layer_out = (mixed + resid.astype(jnp.float32)).astype(jnp.bfloat16)
    rows, cols = layer_out.shape
    wid_n = sizes["wid"]
    wide = exchange(layer_out, *groups.shards, True, 3)
    wide = wide.reshape(wid_n, -1, rows, cols).transpose(0, 2, 1, 3).reshape(wid_n, rows, -1)
    block = exchange(wide, *groups.wid, False, 4).reshape(row_count, -1)
    enc_part = jnp.dot(block, enc_weight, preferred_element_type=jnp.float32)
    preact = scatter_sum(enc_part.astype(jnp.bfloat16), groups.low, 5).astype(jnp.bfloat16)
    preact = scatter_sum(preact, groups.high, 6) + enc_bias
    my_latents = (jax.nn.softplus(4.0 * preact) * 0.25).astype(jnp.bfloat16)
    latents = gather_rows(gather_rows(my_latents, groups.high, 7), groups.low, 8)
    row_scale = row_count ** (-0.5)
    recon = jnp.dot(latents, dec_weight, preferred_element_type=jnp.float32)
    recon = scatter_sum(recon.astype(jnp.bfloat16), groups.shards, 9)
    piece_len = recon.shape[0]
    target = lax.dynamic_slice_in_dim(block, shard_pos * piece_len, piece_len, 0).astype(
        jnp.float32
    )
    scaled_error = ((recon + dec_bias - target) * row_scale).astype(jnp.bfloat16)
    error_all = gather_rows(scaled_error, groups.shards, 10)
    dec_bias_grad = jnp.sum(error_all, axis=0, dtype=jnp.float32)
    latent_part = lax.dot_general(
        error_all, dec_weight, (((1,), (1,)), ((), ())), preferred_element_type=jnp.float32
    )
    dec_grad = lax.dot_general(
        latents, error_all, (((0,), (0,)), ((), ())), preferred_element_type=jnp.float32
    )
    latent_grad = scatter_sum(latent_part.astype(jnp.bfloat16), groups.low, 11).astype(jnp.bfloat16)
    latent_grad = scatter_sum(latent_grad, groups.high, 12)
    my_grad = (latent_grad * jax.nn.sigmoid(4.0 * preact)).astype(jnp.bfloat16)
    preact_grad = gather_rows(gather_rows(my_grad, groups.high, 13), groups.low, 14)
    enc_grad = lax.dot_general(
        block, preact_grad, (((0,), (0,)), ((), ())), preferred_element_type=jnp.float32
    ).astype(jnp.bfloat16)
    enc_bias_grad = jnp.sum(preact_grad, axis=0, dtype=jnp.float32)
    return (layer_out, enc_grad, enc_bias_grad, dec_grad.astype(jnp.bfloat16), dec_bias_grad)


def solution(mesh):
    placed = (
        P(None, "wid", None),
        P(None, ("grp", "ctx"), "wid", None),
        P(None, ("grp", "ctx"), "wid", None),
        P(),
        P(),
        P("wid", ("grp", "ctx")),
        P("wid", ("grp", "ctx")),
        P("wid", ("grp", "ctx")),
        P(("grp", "ctx")),
        P(("grp", "ctx"), "wid"),
        P("wid"),
    )
    return jax.shard_map(
        functools.partial(body, dict(mesh.shape)),
        mesh=mesh,
        in_specs=placed,
        out_specs=(
            P("wid", ("grp", "ctx")),
            P("wid", ("grp", "ctx")),
            P(("grp", "ctx")),
            P(("grp", "ctx"), "wid"),
            P("wid"),
        ),
        check_vma=False,
    )
```

time: 457 us -> 217 us (0.47)
  waiting for transfers between devices: 224 us -> 0 us
  Pallas kernels: 0 us -> 158 us
  blocking collectives: 150 us -> 0 us
  matrix products: 46.2 us -> 31.8 us
  between operations: 13.9 us -> 1.07 us
    pallas_call x0 -> x15, Pallas kernels: none -> 158 us  [exchange(): pl.pallas_call(functools.partial(exchange_kernel, n, where, peer_id, gath...]
    psum x3 -> x0, waiting for transfers between devices: 139 us -> none  [the longest x1 65.7 us: body(): weight_sum, weighted = lax.psum((weight_sum, weighted), ('grp', 'ctx'))]
    reduce_scatter x2 -> x0, waiting for transfers between devices: 85.1 us -> none  [the longest x1 65.3 us: body(): lax.psum_scatter(jnp.dot(latents, dec_weight, preferred_element_type=jnp....]
    all_gather x2 -> x0, blocking collectives: 64.3 us -> none  [the longest x1 32.1 us: body(): wide_rows = lax.all_gather(layer_out, ('grp', 'ctx'), axis=1, tiled=True)]
    pmax x1 -> x0, blocking collectives: 39 us -> none  [body(): peak = lax.pmax(local_peak, ('grp', 'ctx'))]
    psum x1 -> x0, blocking collectives: 34.2 us -> none  [body(): weight_sum, weighted = lax.psum((weight_sum, weighted), ('grp', 'ctx'))]
    all_to_all x1 -> x0, blocking collectives: 12.6 us -> none  [body(): lax.all_to_all(wide_rows, 'wid', split_axis=1, concat_axis=0, tiled=True)]
    dot_general x3, matrix products: 15.6 us -> 8.48 us  [the longest x1 5.99 us: body(): recon = jnp.dot(latents, dec_weight, preferred_element_type=jnp.float32)]
  transfers between devices with their start and end apart: 5 -> 0, of which waited for: 5 -> 0; matrix products, arithmetic and copies ran while one was open for 2% -> 0% of each run, Pallas kernels for 0% -> 0%
where the time goes in v1:
time: 217 us; the launch traced here: 214 us
  Pallas kernels  158 us (73%)
  matrix products  31.8 us (15%)
  other arithmetic  12.1 us (6%)
  local copies, waits for them, and re-layouts  11.3 us (5%)
    pallas_call x15, Pallas kernels, exchange(): pl.pallas_call(functools.partial(exchange_kernel, n, where, peer_id, gath...  158 us
    unnamed x36, local copies, waits for them, and re-layouts  7.41 us
    reduce_sum x6, other arithmetic, scatter_sum(): return jnp.sum(parts.astype(jnp.float32), axis=0)  6 us
    dot_general x1, matrix products, body(): recon = jnp.dot(latents, dec_weight, preferred_element_type=jnp.float32)  5.99 us
    dot_general x1, matrix products, body(): enc_part = jnp.dot(block, enc_weight, preferred_element_type=jnp.float32)  5.73 us
    dot_general x1, matrix products, body(): lax.dot_general(error_all, dec_weight, (((1,), (1,)), ((), ())), preferre...  5.65 us
    dot_general x1, matrix products, body(): lax.dot_general(latents, error_all, (((0,), (0,)), ((), ())), preferred_e...  5.5 us
    dot_general x1, matrix products, body(): lax.dot_general(block, preact_grad, (((0,), (0,)), ((), ())), preferred_e...  5.46 us

profile of v1, /device:TPU:0, one launch (start us, length us, event | category | flops | bytes accessed | tf_op | source)
XLA Modules:
  0.0 214.4 jit_solution(17874746346797019179)
XLA Ops:
  0.7 1.4 maximum_bitcast_fusion
  2.1 10.9 %exchange0.1 = bf16[8,64,256]{2,1,0:T(8,128)(2,1)S(1)} custom-call(bf16[8,64,256]{2,1,0:T(8,128)(2,1)S(1)} %bitcast.67), custom_call_target="tpu_custom_call" | custom-call | tf_op jit(solution)/shard_map/exchange0/pallas_call | solution.py:54
  13.0 2.2 %convolution_multiply_fusion = f32[64,8,512]{2,1,0:T(8,128)} fusion(bf16[512,256]{1,0:T(8,128)(2,1)S(1)} %bitcast.69, bf16[256,16,128]{2,1,0:T(8,128)(2,1)} %param.11, s32[]{:T(128)S(6)} %select_n.51, s32[]{:T(128)S(6)} %select_n.52), kind=kOutput, calls=%fused_computation.15 | convolution fusion | flops 67371008 | bytes 1310728 | tf_op jit(solution)/shard_map/rgd,td->rgt/dot_general | solution.py:125
  16.3 2.1 fusion.19
  18.7 20.8 %exchange1.1 = bf16[8,64,1024]{2,1,0:T(8,128)(2,1)S(1)} custom-call(bf16[64,1024]{1,0:T(8,128)(2,1)S(1)} %bitcast.71), custom_call_target="tpu_custom_call" | custom-call | tf_op jit(solution)/shard_map/exchange1/pallas_call | solution.py:54
  39.6 1.1 copy.22
  42.0 5.6 %exchange2.1 = bf16[4,64,640]{2,1,0:T(8,128)(2,1)S(1)} custom-call(bf16[4,64,640]{2,1,0:T(8,128)(2,1)S(1)} %bitcast.72), custom_call_target="tpu_custom_call" | custom-call | tf_op jit(solution)/shard_map/exchange2/pallas_call | solution.py:54
  47.7 21.4 %exchange3.1 = bf16[8,64,640]{2,1,0:T(8,128)(2,1)S(1)} custom-call(bf16[64,640]{1,0:T(8,128)(2,1)S(1)} %add_convert_fusion.x_ref), custom_call_target="tpu_custom_call" | custom-call | tf_op jit(solution)/shard_map/exchange3/pallas_call | solution.py:54
  69.8 1.3 reshape.135.x_ref
  71.1 1.1 copy-done.9
  72.1 9.0 %exchange4.1 = bf16[4,64,1280]{2,1,0:T(8,128)(2,1)S(1)} custom-call(bf16[4,64,1280]{2,1,0:T(8,128)(2,1)S(1)} %copy-done.9), custom_call_target="tpu_custom_call" | custom-call | tf_op jit(solution)/shard_map/exchange4/pallas_call | solution.py:54
  81.2 5.7 %convolution_convert_fusion.3 = bf16[256,3072]{1,0:T(8,128)(2,1)S(1)} fusion(bf16[256,1280]{1,0:T(8,128)(2,1)S(1)} %bitcast.57, bf16[1280,3072]{1,0:T(8,128)(2,1)} %param.18), kind=kOutput, calls=%fused_computation.4 | convolution fusion | flops 2014052352 | bytes 10092544 | tf_op jit(solution)/shard_map/dot_general | solution.py:167
  86.9 2.9 %exchange5.1 = bf16[2,128,3072]{2,1,0:T(8,128)(2,1)S(1)} custom-call(bf16[2,128,3072]{2,1,0:T(8,128)(2,1)S(1)} %bitcast.65), custom_call_target="tpu_custom_call" | custom-call | tf_op jit(solution)/shard_map/exchange5/pallas_call | solution.py:54
  89.8 1.1 copy-done.4
  91.0 2.8 %reduce_sum.99 = bf16[128,3072]{1,0:T(8,128)(2,1)} reduce(bf16[2,128,3072]{2,1,0:T(8,128)(2,1)} %copy-done.4, bf16[]{:T(256)} %constant.67.clone.1), dimensions={0}, to_apply=%region_4.5 | reduce | flops 393216 | bytes 2359298 | tf_op jit(solution)/shard_map/reduce_sum | solution.py:91
  93.8 1.1 copy-done.8
  94.9 11.4 %exchange6.1 = bf16[2,64,3072]{2,1,0:T(8,128)(2,1)S(1)} custom-call(bf16[2,64,3072]{2,1,0:T(8,128)(2,1)S(1)} %bitcast.61), custom_call_target="tpu_custom_call" | custom-call | tf_op jit(solution)/shard_map/exchange6/pallas_call | solution.py:54
  107.9 10.6 %exchange7.1 = bf16[2,64,3072]{2,1,0:T(8,128)(2,1)S(1)} custom-call(bf16[64,3072]{1,0:T(8,128)(2,1)S(1)} %fusion.11.x_ref), custom_call_target="tpu_custom_call" | custom-call | tf_op jit(solution)/shard_map/exchange7/pallas_call | solution.py:54
  118.5 2.3 %exchange8.1 = bf16[2,128,3072]{2,1,0:T(8,128)(2,1)S(1)} custom-call(bf16[128,3072]{1,0:T(8,128)(2,1)S(1)} %bitcast.62), custom_call_target="tpu_custom_call" | custom-call | tf_op jit(solution)/shard_map/exchange8/pallas_call | solution.py:54
  120.8 6.0 %convolution_convert_fusion.4 = bf16[256,1280]{1,0:T(8,128)(2,1)S(1)} fusion(bf16[256,3072]{1,0:T(8,128)(2,1)S(1)} %bitcast.52, bf16[3072,1280]{1,0:T(8,128)(2,1)} %param.20), kind=kOutput, calls=%fused_computation.6 | convolution fusion | flops 2013593600 | bytes 10092544 | tf_op jit(solution)/shard_map/dot_general | solution.py:173
  126.8 18.8 %exchange9.1 = bf16[8,32,1280]{2,1,0:T(8,128)(2,1)S(1)} custom-call(bf16[8,32,1280]{2,1,0:T(8,128)(2,1)S(1)} %bitcast.68), custom_call_target="tpu_custom_call" | custom-call | tf_op jit(solution)/shard_map/exchange9/pallas_call | solution.py:54
  145.8 18.1 %exchange10.1 = bf16[8,32,1280]{2,1,0:T(8,128)(2,1)S(1)} custom-call(bf16[32,1280]{1,0:T(8,128)(2,1)S(1)} %multiply_convert_fusion.1.x_ref), custom_call_target="tpu_custom_call" | custom-call | tf_op jit(solution)/shard_map/exchange10/pallas_call | solution.py:54
  163.9 5.6 %convolution_convert_fusion.2 = bf16[256,3072]{1,0:T(8,128)(2,1)S(1)} fusion(bf16[256,1280]{1,0:T(8,128)(2,1)S(1)} %bitcast.54, bf16[3072,1280]{1,0:T(8,128)(2,1)} %param.20), kind=kOutput, calls=%fused_computation.3 | convolution fusion | flops 2014052352 | bytes 10092544 | tf_op jit(solution)/shard_map/dot_general | solution.py:182
  169.6 2.3 %exchange11.1 = bf16[2,128,3072]{2,1,0:T(8,128)(2,1)S(1)} custom-call(bf16[2,128,3072]{2,1,0:T(8,128)(2,1)S(1)} %bitcast.66), custom_call_target="tpu_custom_call" | custom-call | tf_op jit(solution)/shard_map/exchange11/pallas_call | solution.py:54
  171.9 1.1 copy-done.3
  173.1 2.8 %reduce_sum.102 = bf16[128,3072]{1,0:T(8,128)(2,1)} reduce(bf16[2,128,3072]{2,1,0:T(8,128)(2,1)} %copy-done.3, bf16[]{:T(256)} %constant.67.clone.1), dimensions={0}, to_apply=%region_7.8 | reduce | flops 393216 | bytes 2359298 | tf_op jit(solution)/shard_map/reduce_sum | solution.py:91
  175.9 1.1 copy-done.7
  177.0 11.2 %exchange12.1 = bf16[2,64,3072]{2,1,0:T(8,128)(2,1)S(1)} custom-call(bf16[2,64,3072]{2,1,0:T(8,128)(2,1)S(1)} %bitcast.60), custom_call_target="tpu_custom_call" | custom-call | tf_op jit(solution)/shard_map/exchange12/pallas_call | solution.py:54
  188.6 10.4 %exchange13.1 = bf16[2,64,3072]{2,1,0:T(8,128)(2,1)S(1)} custom-call(bf16[64,3072]{1,0:T(8,128)(2,1)S(1)} %multiply_convert_fusion.x_ref), custom_call_target="tpu_custom_call" | custom-call | tf_op jit(solution)/shard_map/exchange13/pallas_call | solution.py:54
  199.0 2.3 %exchange14.1 = bf16[2,128,3072]{2,1,0:T(8,128)(2,1)S(1)} custom-call(bf16[128,3072]{1,0:T(8,128)(2,1)S(1)} %bitcast.63), custom_call_target="tpu_custom_call" | custom-call | tf_op jit(solution)/shard_map/exchange14/pallas_call | solution.py:54
  201.3 5.5 %convolution_convert_fusion.1 = bf16[1280,3072]{1,0:T(8,128)(2,1)} fusion(bf16[256,1280]{1,0:T(8,128)(2,1)S(1)} %bitcast.59, bf16[256,3072]{1,0:T(8,128)(2,1)S(1)} %bitcast.51), kind=kOutput, calls=%fused_computation.2 | convolution fusion | flops 2017198080 | bytes 10092544 | tf_op jit(solution)/shard_map/dot_general | solution.py:192
  208.2 5.5 %convolution_convert_fusion = bf16[3072,1280]{1,0:T(8,128)(2,1)} fusion(bf16[256,3072]{1,0:T(8,128)(2,1)S(1)} %bitcast.53, bf16[256,1280]{1,0:T(8,128)(2,1)S(1)} %bitcast.55), kind=kOutput, calls=%fused_computation.1 | convolution fusion | flops 2017198080 | bytes 10092544 | tf_op jit(solution)/shard_map/dot_general | solution.py:185
  (51 shorter events, 7.7 us)
Async XLA Ops:
  0.6 40.3 %copy-start = (bf16[2048,640]{1,0:T(8,128)(2,1)S(1)}, bf16[2048,640]{1,0:T(8,128)(2,1)}, u32[]{:S(2)}) copy-start(bf16[2048,640]{1,0:T(8,128)(2,1)} %param.17) | copy-start | bytes 7864324
  0.6 15.5 %copy-start.16 = (s32[256]{0:T(256)S(1)}, s32[256]{0:T(256)}, u32[]{:S(2)}) copy-start(s32[256]{0:T(256)} %param.15) | copy-start | bytes 3076
  41.0 6.7 %copy-start.13 = (bf16[64,640]{1,0:T(8,128)(2,1)S(1)}, bf16[64,640]{1,0:T(8,128)(2,1)}, u32[]{:S(2)}) copy-start(bf16[64,640]{1,0:T(8,128)(2,1)} %param.16) | copy-start | bytes 245764
  47.7 39.3 %copy-start.10 = (bf16[64,640]{1,0:T(8,128)(2,1)}, bf16[64,640]{1,0:T(8,128)(2,1)S(1)}, u32[]{:S(2)}) copy-start(bf16[64,640]{1,0:T(8,128)(2,1)S(1)} %add_convert_fusion.x_ref) | copy-start | bytes 245764
  71.1 1.1 copy-start.9
  81.2 64.6 %copy-start.5 = (bf16[4,64,1280]{2,1,0:T(8,128)(2,1)}, bf16[4,64,1280]{2,1,0:T(8,128)(2,1)S(1)}, u32[]{:S(2)}) copy-start(bf16[4,64,1280]{2,1,0:T(8,128)(2,1)S(1)} %exchange4.1) | copy-start | bytes 1966084
  89.8 1.1 copy-start.4
  90.9 16.4 %copy-start.14 = (f32[3072]{0:T(1024)S(1)}, f32[3072]{0:T(1024)}, u32[]{:S(2)}) copy-start(f32[3072]{0:T(1024)} %param.19) | copy-start | bytes 36868
  93.8 1.1 copy-start.8
  106.5 0.9 copy-start.11
  120.8 6.0 %copy-start.1 = (bf16[2,128,3072]{2,1,0:T(8,128)(2,1)}, bf16[2,128,3072]{2,1,0:T(8,128)(2,1)S(1)}, u32[]{:S(2)}) copy-start(bf16[2,128,3072]{2,1,0:T(8,128)(2,1)S(1)} %exchange8.1) | copy-start | bytes 4718596
  120.8 24.9 %copy-start.15 = (f32[1280]{0:T(1024)S(1)}, f32[1280]{0:T(1024)}, u32[]{:S(2)}) copy-start(f32[1280]{0:T(1024)} %param.21) | copy-start | bytes 15364
  171.9 1.1 copy-start.3
  175.9 1.1 copy-start.7
  177.0 11.3 %copy-start.12 = (f32[64,3072]{1,0:T(8,128)S(1)}, f32[64,3072]{1,0:T(8,128)}, u32[]{:S(2)}) copy-start(f32[64,3072]{1,0:T(8,128)} %copy-done.11) | copy-start | bytes 2359300
  188.4 13.0 %copy-start.6 = (bf16[4,64,1280]{2,1,0:T(8,128)(2,1)S(1)}, bf16[4,64,1280]{2,1,0:T(8,128)(2,1)}, u32[]{:S(2)}) copy-start(bf16[4,64,1280]{2,1,0:T(8,128)(2,1)} %copy-done.5) | copy-start | bytes 1966084
  206.8 1.4 copy-start.2
